TPU v7x, 128 devices: a whole 4x4x4 slice. The times are simulated.
128 devices in a mesh: dom: 128 (over y, z, x, core).
Axes of the slice: x: 4, y: 4, z: 4, core: 2. Of those that a mesh axis runs over, the one named last changes fastest.
Arguments:
- right_side: float32 [131072, 3], P('dom'), may hold values from -10 to 10
- fine_diagonal: float32 [131072, 3], P('dom'), may hold values from 2 to 4
- fine_columns: int32 [131072, 27], P('dom'), may hold values from 0 to 131071, as said below
- fine_blocks: float32 [131072, 27, 3, 3], P('dom'), may hold values from -0.625 to 0.625
- aggregate_of_node: int32 [131072], P('dom'), may hold values from 0 to 31, as said below
- coarse_row_of_aggregate: int32 [4096], P('dom'), may hold values from 0 to 4095, as said below
- coarse_diagonal: float32 [4096, 3], P('dom'), may hold values from 2 to 4
- coarse_columns: int32 [4096, 27], P('dom'), may hold values from 0 to 4095
- coarse_blocks: float32 [4096, 27, 3, 3], P('dom'), may hold values from -0.625 to 0.625
Outputs:
- solution: float32 [131072, 3], P('dom')
- correction: float32 [4096, 3], P('dom')
Inputs may be any that keep to these rules, and one draw needn't show every extreme that they name: Every entry of fine_columns differs from its row number by at most 256, and some entry by exactly 256. `aggregate_of_node`: on each device every aggregate number 0 to 31 is used by at least one of its nodes. coarse_row_of_aggregate is a permutation of 0 to 4095; among the 32 aggregates of one device (an aligned block of entries) at most 8 get rows of any one owner, and exactly 8 for some owner.
All inputs are finite; a program needn't handle non-finite values.
Results may differ from a plain program's by a relative error of at most 0.0003.
Values sent between devices are 32-bit elements.
A program may use at most 64 MiB of HBM per device.

v0:
```python
import jax
import jax.numpy as jnp
from jax import lax
from jax.sharding import Mesh
from jax.sharding import PartitionSpec as P

CAP = 8
WIN = 256
SWEEPS = 2
CSWEEPS = 6
DOM = ("dom_0", "dom_1", "dom_2", "dom_3")
damping = 0.7
highest = lax.Precision.HIGHEST


def padded_2(value, sides, width, wrap):
    for axis, dim in sides:
        peers, length = (lax.axis_size(axis), value.shape[dim])
        up = [(i, (i + 1) % peers) for i in range(peers if wrap else peers - 1)]
        down = [(j, i) for i, j in up]
        last = lax.slice_in_dim(value, length - width, length, axis=dim)
        initial = lax.slice_in_dim(value, 0, width, axis=dim)
        before = lax.ppermute(last, axis, up)
        after = lax.ppermute(initial, axis, down)
        value = jnp.concatenate([before, value, after], axis=dim)
    return value


def split_up(value, dim, peers):
    return jnp.stack(jnp.split(value, peers, axis=dim))


def joined_along(tiles, dim):
    tiles = jnp.moveaxis(tiles, 0, dim)
    shape = tiles.shape
    return tiles.reshape(*shape[:dim], shape[dim] * shape[dim + 1], *shape[dim + 2 :])


def turned_blocks(tiles, axes, sequence):
    inside = tiles.shape[1:]
    whole = tiles.reshape(*(lax.axis_size(a) for a in axes), *inside)
    for k in sequence:
        whole = lax.all_to_all(whole, axes[k], k, k, tiled=True)
    return whole.reshape(-1, *inside)


def exchange_by_chip(value, groups, sequence, split_dim, concat_dim):
    peers = lax.axis_size(groups[0]) * lax.axis_size(groups[1])
    tiles = split_up(value, split_dim, peers)
    return joined_along(turned_blocks(tiles, groups, sequence), concat_dim)


def couple(blocks, nearby):
    return jnp.sum(blocks * nearby[:, :, None, :], axis=(1, 3))


def apply_fine(field, fine_diagonal, fine_columns, fine_blocks):
    row_count = fine_columns.shape[0]
    padded = padded_2(field, ((DOM, 0),), WIN, False)
    first_row = lax.axis_index(DOM) * row_count - WIN
    local_columns = (fine_columns - first_row).astype(jnp.int32)
    nearby = padded[local_columns]
    return fine_diagonal * field - couple(fine_blocks, nearby)


def apply_coarse(field, coarse_diagonal, coarse_columns, coarse_blocks):
    gathered = lax.all_gather(field, DOM, axis=0, tiled=True)
    nearby = gathered[coarse_columns]
    return coarse_diagonal * field - couple(coarse_blocks, nearby)


def body(
    right_side,
    fine_diagonal,
    fine_columns,
    fine_blocks,
    aggregate_of_node,
    coarse_row_of_aggregate,
    coarse_diagonal,
    coarse_columns,
    coarse_blocks,
):
    solution = damping * right_side / fine_diagonal
    for sweep in range(SWEEPS - 1):
        solution = (
            solution
            + damping
            * (right_side - apply_fine(solution, fine_diagonal, fine_columns, fine_blocks))
            / fine_diagonal
        )
    residual = right_side - apply_fine(solution, fine_diagonal, fine_columns, fine_blocks)
    aggregate_count = coarse_diagonal.shape[0]
    devices = lax.axis_size(DOM)
    aggregate_ids = jnp.arange(aggregate_count, dtype=jnp.int32)
    sums_here = jax.ops.segment_sum(residual, aggregate_of_node, num_segments=aggregate_count)
    owners = coarse_row_of_aggregate // aggregate_count
    member = (owners[:, None] == jnp.arange(devices, dtype=jnp.int32)[None, :]).astype(jnp.float32)
    earlier = (aggregate_ids[None, :] < aggregate_ids[:, None]).astype(jnp.float32)
    before = jnp.dot(earlier, member, precision=highest)
    position = jnp.sum(before * member, axis=1).astype(jnp.int32)
    bucket = (owners * CAP + position).astype(jnp.int32)
    local_rows = (coarse_row_of_aggregate - owners * aggregate_count).astype(jnp.int32)
    slot_out = jnp.full((devices * CAP,), aggregate_count, jnp.int32).at[bucket].set(local_rows)
    slot_in = exchange_by_chip(slot_out, (("dom_0", "dom_1", "dom_2"), "dom_3"), (0, 1), 0, 0)
    outgoing = jnp.zeros((devices * CAP, 3), jnp.float32).at[bucket].set(sums_here)
    arrived = exchange_by_chip(outgoing, (("dom_0", "dom_1", "dom_2"), "dom_3"), (0, 1), 0, 0)
    coarse_rhs = jnp.zeros((aggregate_count, 3), jnp.float32).at[slot_in].add(arrived, mode="drop")
    correction = damping * coarse_rhs / coarse_diagonal
    for sweep in range(CSWEEPS - 1):
        correction = (
            correction
            + damping
            * (
                coarse_rhs
                - apply_coarse(correction, coarse_diagonal, coarse_columns, coarse_blocks)
            )
            / coarse_diagonal
        )
    sending = jnp.take(correction, slot_in, axis=0, mode="fill", fill_value=0.0)
    returned = exchange_by_chip(sending, (("dom_0", "dom_1", "dom_2"), "dom_3"), (0, 1), 0, 0)
    label_values = returned[bucket]
    solution = solution + label_values[aggregate_of_node]
    for sweep in range(SWEEPS):
        solution = (
            solution
            + damping
            * (right_side - apply_fine(solution, fine_diagonal, fine_columns, fine_blocks))
            / fine_diagonal
        )
    return (solution, correction)


def solution(mesh):
    torus = Mesh(mesh.devices.reshape(4, 4, 4, 2), ("dom_0", "dom_1", "dom_2", "dom_3"))
    return jax.shard_map(
        body,
        mesh=torus,
        in_specs=(
            P(DOM, None),
            P(DOM, None),
            P(DOM, None),
            P(DOM, None, None, None),
            P(DOM),
            P(DOM),
            P(DOM, None),
            P(DOM, None),
            P(DOM, None, None, None),
        ),
        out_specs=(P(DOM, None), P(DOM, None)),
        check_vma=False,
    )
```

profile of v0, /device:TPU:103, one launch (start us, length us, event | category | flops | bytes accessed | tf_op | source)
XLA Modules:
  0.0 762.8 jit_solution(1142505852747501974)
XLA Ops:
  1.4 2.3 collective-permute-start
  3.7 2.2 collective-permute-start.1
  8.2 9.7 %stack.1289 = s32[128,8]{1,0:T(8,128)} concatenate(s32[1,8]{1,0:T(1,128)S(1)} %get-tuple-element.405, s32[1,8]{1,0:T(1,128)S(1)} %get-tuple-element.404, s32[1,8]{1,0:T(1,128)S(1)} %get-tuple-element.403, s32[1,8]{1,0:T(1,128)S(1)} %get-tuple-element.402, s32[1,8]{1,0:T(1,128)S(1)} %get-tuple-element.401, s32[1,8]{1,0:T(1,128)S(1)} %get-tuple-element.400, ...), dimensions={0} | concatenate | bytes 8192 | tf_op jit(solution)/shard_map/stack | solution.py:30
  17.9 10.3 %all-to-all-start = ((s32[64,2,8]{2,1,0:T(2,128)}), s32[64,2,8]{2,1,0:T(2,128)S(1)}, u32[]{:S(2)}, u32[]{:S(2)}) async-start(s32[64,2,8]{2,1,0:T(2,128)} %bitcast.128), calls=%async_computation | async-start | bytes 131072 | tf_op jit(solution)/shard_map/all_to_all | solution.py:43
  30.3 91.5 %gather_fusion = f32[27648,3]{1,0:T(8,128)} fusion(f32[1536,3]{1,0:T(8,128)S(1)} %copy.2716, s32[27648]{0:T(1024)S(1)} %broadcast_clamp_fusion), kind=kCustom, calls=%fused_computation | custom fusion | bytes 774144 | tf_op jit(solution)/shard_map/gather | solution.py:62
  121.8 8.3 %copy.2717 = f32[27648,3]{0,1:T(4,128)S(1)} copy(f32[27648,3]{1,0:T(8,128)} %gather_fusion) | data formatting | bytes 663552 | tf_op jit(solution)/shard_map/gather | solution.py:62
  130.1 3.0 reshape.61
  133.1 1.9 copy.2718
  135.2 4.5 collective-permute-start.2
  139.7 1.9 collective-permute-start.3
  141.8 4.0 all_to_all.30
  149.1 91.5 %gather_fusion.1 = f32[27648,3]{1,0:T(8,128)} fusion(f32[1536,3]{1,0:T(8,128)S(1)} %copy.2722, s32[27648]{0:T(1024)S(1)} %broadcast_clamp_fusion), kind=kCustom, calls=%fused_computation.1 | custom fusion | bytes 774144 | tf_op jit(solution)/shard_map/gather | solution.py:62
  240.7 8.3 %copy.2723 = f32[27648,3]{0,1:T(4,128)S(1)} copy(f32[27648,3]{1,0:T(8,128)} %gather_fusion.1) | data formatting | bytes 663552 | tf_op jit(solution)/shard_map/gather | solution.py:62
  248.9 3.0 reshape.69
  251.9 1.9 copy.2724
  254.3 6.0 scatter_custom_fusion.1
  274.1 8.9 %all-to-all-start.2 = ((f32[64,2,8,3]{2,1,3,0:T(2,128)}), f32[64,2,8,3]{2,1,3,0:T(2,128)S(1)}, u32[]{:S(2)}, u32[]{:S(2)}) async-start(f32[64,2,8,3]{2,1,3,0:T(2,128)} %copy.2855), calls=%async_computation.2 | async-start | bytes 393216 | tf_op jit(solution)/shard_map/all_to_all | solution.py:43
  283.1 6.5 all-to-all-done.2
  289.7 4.9 all_to_all.31
  296.2 6.0 scatter_custom_fusion.3
  302.3 34.5 %all-gather = f32[128,32,3]{1,2,0:T(4,128)S(1)} all-gather(f32[1,32,3]{1,2,0:T(4,128)S(1)} %fusion.11), channel_id=1, replica_groups=mesh['dom_0'=4,'dom_1'=4,'dom_2'=4,'dom_3'=2] {'dom_0','dom_1','dom_2','..., dimensions={0}, use_global_device_ids=true | all-gather | bytes 49536 | tf_op jit(solution)/shard_map/all_gather | solution.py:67
  337.7 1.9 gather_fusion.2
  340.0 33.4 %all-gather.1 = f32[128,32,3]{1,2,0:T(4,128)S(1)} all-gather(f32[1,32,3]{1,2,0:T(4,128)S(1)} %bitcast.827), channel_id=1, replica_groups=mesh['dom_0'=4,'dom_1'=4,'dom_2'=4,'dom_3'=2] {'dom_0','dom_1','dom_2','..., dimensions={0}, use_global_device_ids=true | all-gather | bytes 49536 | tf_op jit(solution)/shard_map/all_gather | solution.py:67
  374.2 1.9 gather_fusion.3
  376.5 33.4 %all-gather.2 = f32[128,32,3]{1,2,0:T(4,128)S(1)} all-gather(f32[1,32,3]{1,2,0:T(4,128)S(1)} %bitcast.825), channel_id=1, replica_groups=mesh['dom_0'=4,'dom_1'=4,'dom_2'=4,'dom_3'=2] {'dom_0','dom_1','dom_2','..., dimensions={0}, use_global_device_ids=true | all-gather | bytes 49536 | tf_op jit(solution)/shard_map/all_gather | solution.py:67
  410.7 1.9 gather_fusion.4
  413.0 33.6 %all-gather.3 = f32[128,32,3]{1,2,0:T(4,128)S(1)} all-gather(f32[1,32,3]{1,2,0:T(4,128)S(1)} %bitcast.826), channel_id=1, replica_groups=mesh['dom_0'=4,'dom_1'=4,'dom_2'=4,'dom_3'=2] {'dom_0','dom_1','dom_2','..., dimensions={0}, use_global_device_ids=true | all-gather | bytes 49536 | tf_op jit(solution)/shard_map/all_gather | solution.py:67
  447.5 1.9 gather_fusion.5
  449.8 33.4 %all-gather.4 = f32[128,32,3]{1,2,0:T(4,128)S(1)} all-gather(f32[1,32,3]{1,2,0:T(4,128)S(1)} %bitcast.824), channel_id=1, replica_groups=mesh['dom_0'=4,'dom_1'=4,'dom_2'=4,'dom_3'=2] {'dom_0','dom_1','dom_2','..., dimensions={0}, use_global_device_ids=true | all-gather | bytes 49536 | tf_op jit(solution)/shard_map/all_gather | solution.py:67
  486.4 2.8 gather_fusion.7
  502.2 7.5 all-to-all-start.4
  509.8 6.3 all-to-all-done.4
  516.3 5.0 all_to_all.32
  523.0 2.8 gather_fusion.9
  526.0 5.5 collective-permute-start.4
  531.5 1.9 collective-permute-start.5
  533.5 7.2 collective-permute-done.5
  541.0 91.5 %gather_fusion.10 = f32[27648,3]{1,0:T(8,128)} fusion(f32[1536,3]{1,0:T(8,128)S(1)} %copy.3009, s32[27648]{0:T(1024)S(1)} %broadcast_clamp_fusion), kind=kCustom, calls=%fused_computation.10 | custom fusion | bytes 774144 | tf_op jit(solution)/shard_map/gather | solution.py:62
  632.5 8.3 %copy.3010 = f32[27648,3]{0,1:T(4,128)S(1)} copy(f32[27648,3]{1,0:T(8,128)} %gather_fusion.10) | data formatting | bytes 663552 | tf_op jit(solution)/shard_map/gather | solution.py:62
  640.8 3.0 reshape.141
  643.8 1.9 copy.3011
  645.9 1.9 collective-permute-start.6
  647.8 2.6 collective-permute-start.7
  650.5 6.5 collective-permute-done.7
  657.3 91.5 %gather_fusion.11 = f32[27648,3]{1,0:T(8,128)} fusion(f32[1536,3]{1,0:T(8,128)S(1)} %copy.3012, s32[27648]{0:T(1024)S(1)} %broadcast_clamp_fusion), kind=kCustom, calls=%fused_computation.11 | custom fusion | bytes 774144 | tf_op jit(solution)/shard_map/gather | solution.py:62
  748.8 8.3 %copy.3013 = f32[27648,3]{0,1:T(4,128)S(1)} copy(f32[27648,3]{1,0:T(8,128)} %gather_fusion.11) | data formatting | bytes 663552 | tf_op jit(solution)/shard_map/gather | solution.py:62
  757.1 3.0 reshape.149
  760.1 1.9 copy.3014
  (650 shorter events, 48.6 us)
Async XLA Ops:
  0.6 29.2 %copy-start.6 = (s32[32,27]{1,0:T(8,128)S(1)}, s32[32,27]{1,0:T(8,128)}, u32[]{:S(2)}) copy-start(s32[32,27]{1,0:T(8,128)} %param.16) | copy-start | bytes 10372
  1.4 28.5 %collective-permute-start = (f32[256,3]{0,1:T(4,128)S(1)}, f32[256,3]{0,1:T(4,128)S(1)}, u32[]{:S(2)}, u32[]{:S(2)}) collective-permute-start(f32[256,3]{0,1:T(4,128)S(1)} %get-tuple-element.276), channel_id=1, source_target_pairs={{0,1},{1,2},{2,3},{3,4},{4,5},{5,6},{6,7},{7,8},{8,9},{9,10},{10,1... | collective-permute-start | bytes 9224 | tf_op jit(solution)/shard_map/ppermute | solution.py:23
  3.7 26.2 %collective-permute-start.1 = (f32[256,3]{0,1:T(4,128)S(1)}, f32[256,3]{0,1:T(4,128)S(1)}, u32[]{:S(2)}, u32[]{:S(2)}) collective-permute-start(f32[256,3]{0,1:T(4,128)S(1)} %get-tuple-element.277), channel_id=1, source_target_pairs={{1,0},{2,1},{3,2},{4,3},{5,4},{6,5},{7,6},{8,7},{9,8},{10,9},{11,1... | collective-permute-start | bytes 9224 | tf_op jit(solution)/shard_map/ppermute | solution.py:24
  17.9 123.7 %all-to-all-start = ((s32[64,2,8]{2,1,0:T(2,128)}), s32[64,2,8]{2,1,0:T(2,128)S(1)}, u32[]{:S(2)}, u32[]{:S(2)}) async-start(s32[64,2,8]{2,1,0:T(2,128)} %bitcast.128), calls=%async_computation | async-start | bytes 131072 | tf_op jit(solution)/shard_map/all_to_all | solution.py:43
  130.1 4.9 copy-start
  133.1 2.1 copy-start.3
  133.1 2.1 copy-start.4
  135.2 12.3 %collective-permute-start.2 = (f32[256,3]{0,1:T(4,128)S(1)}, f32[256,3]{0,1:T(4,128)S(1)}, u32[]{:S(2)}, u32[]{:S(2)}) collective-permute-start(f32[256,3]{0,1:T(4,128)S(1)} %get-tuple-element.274), channel_id=1, source_target_pairs={{0,1},{1,2},{2,3},{3,4},{4,5},{5,6},{6,7},{7,8},{8,9},{9,10},{10,1... | collective-permute-start | bytes 9224 | tf_op jit(solution)/shard_map/ppermute | solution.py:23
  139.7 9.1 %collective-permute-start.3 = (f32[256,3]{0,1:T(4,128)S(1)}, f32[256,3]{0,1:T(4,128)S(1)}, u32[]{:S(2)}, u32[]{:S(2)}) collective-permute-start(f32[256,3]{0,1:T(4,128)S(1)} %get-tuple-element.275), channel_id=1, source_target_pairs={{1,0},{2,1},{3,2},{4,3},{5,4},{6,5},{7,6},{8,7},{9,8},{10,9},{11,1... | collective-permute-start | bytes 9224 | tf_op jit(solution)/shard_map/ppermute | solution.py:24
  251.9 2.3 copy-start.8
  261.3 41.0 %copy-start.5 = (f32[32,3]{0,1:T(4,128)S(1)}, f32[32,3]{0,1:T(4,128)}, u32[]{:S(2)}) copy-start(f32[32,3]{0,1:T(4,128)} %param.15) | copy-start | bytes 1156
  274.1 15.4 %all-to-all-start.2 = ((f32[64,2,8,3]{2,1,3,0:T(2,128)}), f32[64,2,8,3]{2,1,3,0:T(2,128)S(1)}, u32[]{:S(2)}, u32[]{:S(2)}) async-start(f32[64,2,8,3]{2,1,3,0:T(2,128)} %copy.2855), calls=%async_computation.2 | async-start | bytes 393216 | tf_op jit(solution)/shard_map/all_to_all | solution.py:43
  337.7 2.2 copy-start.2
  486.3 2.9 copy-start.7
  502.2 13.8 %all-to-all-start.4 = ((f32[64,2,8,3]{2,1,3,0:T(2,128)}), f32[64,2,8,3]{2,1,3,0:T(2,128)S(1)}, u32[]{:S(2)}, u32[]{:S(2)}) async-start(f32[64,2,8,3]{2,1,3,0:T(2,128)} %copy.3005), calls=%async_computation.4 | async-start | bytes 393216 | tf_op jit(solution)/shard_map/all_to_all | solution.py:43
  526.0 7.4 collective-permute-start.4
  531.5 9.1 %collective-permute-start.5 = (f32[256,3]{0,1:T(4,128)S(1)}, f32[256,3]{0,1:T(4,128)S(1)}, u32[]{:S(2)}, u32[]{:S(2)}) collective-permute-start(f32[256,3]{0,1:T(4,128)S(1)} %get-tuple-element.273), channel_id=1, source_target_pairs={{1,0},{2,1},{3,2},{4,3},{5,4},{6,5},{7,6},{8,7},{9,8},{10,9},{11,1... | collective-permute-start | bytes 9224 | tf_op jit(solution)/shard_map/ppermute | solution.py:24
  640.8 4.9 copy-start.1
  645.9 4.6 collective-permute-start.6
  647.8 9.1 %collective-permute-start.7 = (f32[256,3]{0,1:T(4,128)S(1)}, f32[256,3]{0,1:T(4,128)S(1)}, u32[]{:S(2)}, u32[]{:S(2)}) collective-permute-start(f32[256,3]{0,1:T(4,128)S(1)} %get-tuple-element.271), channel_id=1, source_target_pairs={{1,0},{2,1},{3,2},{4,3},{5,4},{6,5},{7,6},{8,7},{9,8},{10,9},{11,1... | collective-permute-start | bytes 9224 | tf_op jit(solution)/shard_map/ppermute | solution.py:24
where the time goes:
time: 764 us; the launch traced here: 763 us
  local copies, waits for them, and re-layouts  482 us (63%)
  blocking collectives  182 us (24%)
  starting transfers between devices  49.7 us (7%)
  waiting for transfers between devices  27.8 us (4%)
  other arithmetic  18.7 us (2%)
    gather x16, local copies, waits for them, and re-layouts, apply_fine(): nearby = padded[local_columns]  419 us
    all_gather x5, blocking collectives, apply_coarse(): gathered = lax.all_gather(field, DOM, axis=0, tiled=True)  168 us
    all_to_all x3, starting transfers between devices, turned_blocks(): whole = lax.all_to_all(whole, axes[k], k, k, tiled=True)  26.8 us
    split x270, local copies, waits for them, and re-layouts, split_up(): return jnp.stack(jnp.split(value, peers, axis=dim))  20.8 us
  transfers between devices with their start and end apart: 11, of which 5 were waited for; matrix products, arithmetic and copies ran while one was open for 16% of the time, Pallas kernels for 0%

commit v1 on v0

--- a/solution.py
+++ b/solution.py
@@ -64,7 +64,9 @@
 
 
 def apply_coarse(field, coarse_diagonal, coarse_columns, coarse_blocks):
-    gathered = lax.all_gather(field, DOM, axis=0, tiled=True)
+    gathered = jnp.concatenate(
+        lax.all_to_all(jnp.stack([field] * lax.axis_size(DOM)), DOM, 0, 0), axis=0
+    )
     nearby = gathered[coarse_columns]
     return coarse_diagonal * field - couple(coarse_blocks, nearby)
 

time: 764 us -> 675 us (0.88)
  blocking collectives: 182 us -> 45.2 us
  starting transfers between devices: 49.7 us -> 74.8 us
  waiting for transfers between devices: 27.8 us -> 48.4 us
    all_gather x5 -> x0, blocking collectives: 168 us -> none  [apply_coarse(): gathered = lax.all_gather(field, DOM, axis=0, tiled=True)]
    all_to_all x0 -> x2, blocking collectives: none -> 30.6 us  [apply_coarse(): lax.all_to_all(jnp.stack([field] * lax.axis_size(DOM)), DOM, 0, 0)]
    all_to_all x0 -> x3, starting transfers between devices: none -> 25 us  [apply_coarse(): lax.all_to_all(jnp.stack([field] * lax.axis_size(DOM)), DOM, 0, 0)]
    all_to_all x0 -> x3, waiting for transfers between devices: none -> 20.5 us  [apply_coarse(): lax.all_to_all(jnp.stack([field] * lax.axis_size(DOM)), DOM, 0, 0)]
  transfers between devices with their start and end apart: 11 -> 14, of which waited for: 5 -> 8; matrix products, arithmetic and copies ran while one was open for 16% -> 18% of each run, Pallas kernels for 0% -> 0%
where the time goes in v1:
time: 675 us; the launch traced here: 674 us
  local copies, waits for them, and re-layouts  484 us (72%)
  starting transfers between devices  74.8 us (11%)
  waiting for transfers between devices  48.4 us (7%)
  blocking collectives  45.2 us (7%)
  other arithmetic  18.7 us (3%)
    gather x16, local copies, waits for them, and re-layouts, apply_fine(): nearby = padded[local_columns]  418 us
    all_to_all x2, blocking collectives, apply_coarse(): lax.all_to_all(jnp.stack([field] * lax.axis_size(DOM)), DOM, 0, 0)  30.6 us
    all_to_all x3, starting transfers between devices, turned_blocks(): whole = lax.all_to_all(whole, axes[k], k, k, tiled=True)  26.9 us
    all_to_all x3, starting transfers between devices, apply_coarse(): lax.all_to_all(jnp.stack([field] * lax.axis_size(DOM)), DOM, 0, 0)  25 us
    split x270, local copies, waits for them, and re-layouts, split_up(): return jnp.stack(jnp.split(value, peers, axis=dim))  20.8 us
    all_to_all x3, waiting for transfers between devices, apply_coarse(): lax.all_to_all(jnp.stack([field] * lax.axis_size(DOM)), DOM, 0, 0)  20.5 us
    ppermute x4, waiting for transfers between devices, padded_2(): after = lax.ppermute(initial, axis, down)  15.1 us
    all_to_all x3, blocking collectives, turned_blocks(): whole = lax.all_to_all(whole, axes[k], k, k, tiled=True)  14.6 us
  transfers between devices with their start and end apart: 14, of which 8 were waited for; matrix products, arithmetic and copies ran while one was open for 18% of the time, Pallas kernels for 0%

profile of v1, /device:TPU:103, one launch (start us, length us, event | category | flops | bytes accessed | tf_op | source)
XLA Modules:
  0.0 673.5 jit_solution(5358940583372504667)
XLA Ops:
  1.4 2.3 collective-permute-start
  3.7 2.2 collective-permute-start.1
  8.2 9.7 %stack.912 = s32[128,8]{1,0:T(8,128)} concatenate(s32[1,8]{1,0:T(1,128)S(1)} %get-tuple-element.405, s32[1,8]{1,0:T(1,128)S(1)} %get-tuple-element.404, s32[1,8]{1,0:T(1,128)S(1)} %get-tuple-element.403, s32[1,8]{1,0:T(1,128)S(1)} %get-tuple-element.402, s32[1,8]{1,0:T(1,128)S(1)} %get-tuple-element.401, s32[1,8]{1,0:T(1,128)S(1)} %get-tuple-element.400, ...), dimensions={0} | concatenate | bytes 8192 | tf_op jit(solution)/shard_map/stack | solution.py:30
  17.9 10.3 %all-to-all-start = ((s32[64,2,8]{2,1,0:T(2,128)}), s32[64,2,8]{2,1,0:T(2,128)S(1)}, u32[]{:S(2)}, u32[]{:S(2)}) async-start(s32[64,2,8]{2,1,0:T(2,128)} %bitcast.128), calls=%async_computation | async-start | bytes 131072 | tf_op jit(solution)/shard_map/all_to_all | solution.py:43
  30.1 91.5 %gather_fusion = f32[27648,3]{1,0:T(8,128)} fusion(f32[1536,3]{1,0:T(8,128)S(1)} %copy.2696, s32[27648]{0:T(1024)S(1)} %broadcast_clamp_fusion), kind=kCustom, calls=%fused_computation | custom fusion | bytes 774144 | tf_op jit(solution)/shard_map/gather | solution.py:62
  121.6 8.3 %copy.2697 = f32[27648,3]{0,1:T(4,128)S(1)} copy(f32[27648,3]{1,0:T(8,128)} %gather_fusion) | data formatting | bytes 663552 | tf_op jit(solution)/shard_map/gather | solution.py:62
  129.8 3.0 reshape.91
  132.8 1.9 copy.2698
  135.0 4.5 collective-permute-start.2
  139.5 1.9 collective-permute-start.3
  141.7 4.0 all_to_all.55
  148.9 91.5 %gather_fusion.1 = f32[27648,3]{1,0:T(8,128)} fusion(f32[1536,3]{1,0:T(8,128)S(1)} %copy.2702, s32[27648]{0:T(1024)S(1)} %broadcast_clamp_fusion), kind=kCustom, calls=%fused_computation.1 | custom fusion | bytes 774144 | tf_op jit(solution)/shard_map/gather | solution.py:62
  240.4 8.3 %copy.2703 = f32[27648,3]{0,1:T(4,128)S(1)} copy(f32[27648,3]{1,0:T(8,128)} %gather_fusion.1) | data formatting | bytes 663552 | tf_op jit(solution)/shard_map/gather | solution.py:62
  248.6 3.0 reshape.99
  251.6 1.9 copy.2704
  253.9 6.0 scatter_custom_fusion.1
  273.8 8.9 %all-to-all-start.2 = ((f32[64,2,8,3]{2,1,3,0:T(2,128)}), f32[64,2,8,3]{2,1,3,0:T(2,128)S(1)}, u32[]{:S(2)}, u32[]{:S(2)}) async-start(f32[64,2,8,3]{2,1,3,0:T(2,128)} %copy.2835), calls=%async_computation.2 | async-start | bytes 393216 | tf_op jit(solution)/shard_map/all_to_all | solution.py:43
  282.7 6.5 all-to-all-done.2
  289.4 4.8 all_to_all.56
  295.9 6.0 scatter_custom_fusion.3
  302.7 7.8 %all-to-all-start.4 = ((f32[128,32,3]{1,2,0:T(4,128)}), f32[128,32,3]{1,2,0:T(4,128)S(1)}, u32[]{:S(2)}, u32[]{:S(2)}) async-start(f32[128,32,3]{1,2,0:T(4,128)} %stack.2074), calls=%async_computation.4 | async-start | bytes 524288 | tf_op jit(solution)/shard_map/all_to_all | solution.py:68
  310.6 6.9 %all-to-all-done.4 = f32[128,32,3]{1,2,0:T(4,128)S(1)} async-done(((f32[128,32,3]{1,2,0:T(4,128)}), f32[128,32,3]{1,2,0:T(4,128)S(1)}, u32[]{:S(2)}, u32[]{:S(2)}) %all-to-all-start.4) | async-done | bytes 49184 | tf_op jit(solution)/shard_map/all_to_all | solution.py:68
  318.3 1.9 gather_fusion.2
  320.7 15.3 %all_to_all.57 = f32[128,32,3]{1,2,0:T(4,128)S(1)} all-to-all(f32[128,32,3]{1,2,0:T(4,128)S(1)} %stack.2075), channel_id=1, replica_groups=mesh['dom_0'=4,'dom_1'=4,'dom_2'=4,'dom_3'=2] {'dom_0','dom_1','dom_2','..., dimensions={0} | all-to-all | bytes 98304 | tf_op jit(solution)/shard_map/all_to_all | solution.py:68
  339.2 15.3 %all_to_all.58 = f32[128,32,3]{1,2,0:T(4,128)S(1)} all-to-all(f32[128,32,3]{1,2,0:T(4,128)S(1)} %stack.2076), channel_id=1, replica_groups=mesh['dom_0'=4,'dom_1'=4,'dom_2'=4,'dom_3'=2] {'dom_0','dom_1','dom_2','..., dimensions={0} | all-to-all | bytes 98304 | tf_op jit(solution)/shard_map/all_to_all | solution.py:68
  358.4 8.6 %all-to-all-start.7 = ((f32[128,32,3]{1,2,0:T(4,128)}), f32[128,32,3]{1,2,0:T(4,128)S(1)}, u32[]{:S(2)}, u32[]{:S(2)}) async-start(f32[128,32,3]{1,2,0:T(4,128)} %stack.2077), calls=%async_computation.7 | async-start | bytes 524288 | tf_op jit(solution)/shard_map/all_to_all | solution.py:68
  367.1 6.8 %all-to-all-done.7 = f32[128,32,3]{1,2,0:T(4,128)S(1)} async-done(((f32[128,32,3]{1,2,0:T(4,128)}), f32[128,32,3]{1,2,0:T(4,128)S(1)}, u32[]{:S(2)}, u32[]{:S(2)}) %all-to-all-start.7) | async-done | bytes 49184 | tf_op jit(solution)/shard_map/all_to_all | solution.py:68
  377.7 8.6 %all-to-all-start.8 = ((f32[128,32,3]{1,2,0:T(4,128)}), f32[128,32,3]{1,2,0:T(4,128)S(1)}, u32[]{:S(2)}, u32[]{:S(2)}) async-start(f32[128,32,3]{1,2,0:T(4,128)} %stack.2078), calls=%async_computation.8 | async-start | bytes 524288 | tf_op jit(solution)/shard_map/all_to_all | solution.py:68
  386.3 6.9 %all-to-all-done.8 = f32[128,32,3]{1,2,0:T(4,128)S(1)} async-done(((f32[128,32,3]{1,2,0:T(4,128)}), f32[128,32,3]{1,2,0:T(4,128)S(1)}, u32[]{:S(2)}, u32[]{:S(2)}) %all-to-all-start.8) | async-done | bytes 49184 | tf_op jit(solution)/shard_map/all_to_all | solution.py:68
  396.5 2.8 gather_fusion.7
  412.3 7.7 %all-to-all-start.9 = ((f32[64,2,8,3]{2,1,3,0:T(2,128)}), f32[64,2,8,3]{2,1,3,0:T(2,128)S(1)}, u32[]{:S(2)}, u32[]{:S(2)}) async-start(f32[64,2,8,3]{2,1,3,0:T(2,128)} %copy.2985), calls=%async_computation.9 | async-start | bytes 393216 | tf_op jit(solution)/shard_map/all_to_all | solution.py:43
  420.0 6.3 all-to-all-done.9
  426.5 5.8 all_to_all.59
  433.9 2.8 gather_fusion.9
  437.0 5.5 collective-permute-start.4
  442.4 1.9 collective-permute-start.5
  444.4 7.2 %collective-permute-done.5 = f32[256,3]{0,1:T(4,128)S(1)} collective-permute-done((f32[256,3]{0,1:T(4,128)S(1)}, f32[256,3]{0,1:T(4,128)S(1)}, u32[]{:S(2)}, u32[]{:S(2)}) %collective-permute-start.5) | collective-permute-done | bytes 3104 | tf_op jit(solution)/shard_map/ppermute | solution.py:24
  451.9 91.5 %gather_fusion.10 = f32[27648,3]{1,0:T(8,128)} fusion(f32[1536,3]{1,0:T(8,128)S(1)} %copy.2989, s32[27648]{0:T(1024)S(1)} %broadcast_clamp_fusion), kind=kCustom, calls=%fused_computation.10 | custom fusion | bytes 774144 | tf_op jit(solution)/shard_map/gather | solution.py:62
  543.3 8.3 %copy.2990 = f32[27648,3]{0,1:T(4,128)S(1)} copy(f32[27648,3]{1,0:T(8,128)} %gather_fusion.10) | data formatting | bytes 663552 | tf_op jit(solution)/shard_map/gather | solution.py:62
  551.6 3.0 reshape.171
  554.6 1.9 copy.2991
  556.7 1.9 collective-permute-start.6
  558.7 2.6 collective-permute-start.7
  561.3 6.5 collective-permute-done.7
  568.1 91.5 %gather_fusion.11 = f32[27648,3]{1,0:T(8,128)} fusion(f32[1536,3]{1,0:T(8,128)S(1)} %copy.2992, s32[27648]{0:T(1024)S(1)} %broadcast_clamp_fusion), kind=kCustom, calls=%fused_computation.11 | custom fusion | bytes 774144 | tf_op jit(solution)/shard_map/gather | solution.py:62
  659.6 8.3 %copy.2993 = f32[27648,3]{0,1:T(4,128)S(1)} copy(f32[27648,3]{1,0:T(8,128)} %gather_fusion.11) | data formatting | bytes 663552 | tf_op jit(solution)/shard_map/gather | solution.py:62
  667.8 3.0 reshape.179
  670.8 1.9 copy.2994
  (658 shorter events, 56.5 us)
Async XLA Ops:
  1.4 28.4 %collective-permute-start = (f32[256,3]{0,1:T(4,128)S(1)}, f32[256,3]{0,1:T(4,128)S(1)}, u32[]{:S(2)}, u32[]{:S(2)}) collective-permute-start(f32[256,3]{0,1:T(4,128)S(1)} %get-tuple-element.276), channel_id=1, source_target_pairs={{0,1},{1,2},{2,3},{3,4},{4,5},{5,6},{6,7},{7,8},{8,9},{9,10},{10,1... | collective-permute-start | bytes 9224 | tf_op jit(solution)/shard_map/ppermute | solution.py:23
  3.7 26.1 %collective-permute-start.1 = (f32[256,3]{0,1:T(4,128)S(1)}, f32[256,3]{0,1:T(4,128)S(1)}, u32[]{:S(2)}, u32[]{:S(2)}) collective-permute-start(f32[256,3]{0,1:T(4,128)S(1)} %get-tuple-element.277), channel_id=1, source_target_pairs={{1,0},{2,1},{3,2},{4,3},{5,4},{6,5},{7,6},{8,7},{9,8},{10,9},{11,1... | collective-permute-start | bytes 9224 | tf_op jit(solution)/shard_map/ppermute | solution.py:24
  17.9 123.6 %all-to-all-start = ((s32[64,2,8]{2,1,0:T(2,128)}), s32[64,2,8]{2,1,0:T(2,128)S(1)}, u32[]{:S(2)}, u32[]{:S(2)}) async-start(s32[64,2,8]{2,1,0:T(2,128)} %bitcast.128), calls=%async_computation | async-start | bytes 131072 | tf_op jit(solution)/shard_map/all_to_all | solution.py:43
  129.8 4.9 copy-start
  132.8 2.1 copy-start.3
  132.8 2.1 copy-start.4
  132.8 8.6 %copy-start.6 = (s32[32,27]{1,0:T(8,128)S(1)}, s32[32,27]{1,0:T(8,128)}, u32[]{:S(2)}) copy-start(s32[32,27]{1,0:T(8,128)} %param.16) | copy-start | bytes 10372
  135.0 12.2 %collective-permute-start.2 = (f32[256,3]{0,1:T(4,128)S(1)}, f32[256,3]{0,1:T(4,128)S(1)}, u32[]{:S(2)}, u32[]{:S(2)}) collective-permute-start(f32[256,3]{0,1:T(4,128)S(1)} %get-tuple-element.274), channel_id=1, source_target_pairs={{0,1},{1,2},{2,3},{3,4},{4,5},{5,6},{6,7},{7,8},{8,9},{9,10},{10,1... | collective-permute-start | bytes 9224 | tf_op jit(solution)/shard_map/ppermute | solution.py:23
  139.5 9.1 %collective-permute-start.3 = (f32[256,3]{0,1:T(4,128)S(1)}, f32[256,3]{0,1:T(4,128)S(1)}, u32[]{:S(2)}, u32[]{:S(2)}) collective-permute-start(f32[256,3]{0,1:T(4,128)S(1)} %get-tuple-element.275), channel_id=1, source_target_pairs={{1,0},{2,1},{3,2},{4,3},{5,4},{6,5},{7,6},{8,7},{9,8},{10,9},{11,1... | collective-permute-start | bytes 9224 | tf_op jit(solution)/shard_map/ppermute | solution.py:24
  251.6 2.3 copy-start.8
  261.0 41.0 %copy-start.5 = (f32[32,3]{0,1:T(4,128)S(1)}, f32[32,3]{0,1:T(4,128)}, u32[]{:S(2)}) copy-start(f32[32,3]{0,1:T(4,128)} %param.15) | copy-start | bytes 1156
  273.8 15.4 %all-to-all-start.2 = ((f32[64,2,8,3]{2,1,3,0:T(2,128)}), f32[64,2,8,3]{2,1,3,0:T(2,128)S(1)}, u32[]{:S(2)}, u32[]{:S(2)}) async-start(f32[64,2,8,3]{2,1,3,0:T(2,128)} %copy.2835), calls=%async_computation.2 | async-start | bytes 393216 | tf_op jit(solution)/shard_map/all_to_all | solution.py:43
  302.7 14.7 %all-to-all-start.4 = ((f32[128,32,3]{1,2,0:T(4,128)}), f32[128,32,3]{1,2,0:T(4,128)S(1)}, u32[]{:S(2)}, u32[]{:S(2)}) async-start(f32[128,32,3]{1,2,0:T(4,128)} %stack.2074), calls=%async_computation.4 | async-start | bytes 524288 | tf_op jit(solution)/shard_map/all_to_all | solution.py:68
  318.3 2.2 copy-start.2
  358.4 15.5 %all-to-all-start.7 = ((f32[128,32,3]{1,2,0:T(4,128)}), f32[128,32,3]{1,2,0:T(4,128)S(1)}, u32[]{:S(2)}, u32[]{:S(2)}) async-start(f32[128,32,3]{1,2,0:T(4,128)} %stack.2077), calls=%async_computation.7 | async-start | bytes 524288 | tf_op jit(solution)/shard_map/all_to_all | solution.py:68
  377.7 15.5 %all-to-all-start.8 = ((f32[128,32,3]{1,2,0:T(4,128)}), f32[128,32,3]{1,2,0:T(4,128)S(1)}, u32[]{:S(2)}, u32[]{:S(2)}) async-start(f32[128,32,3]{1,2,0:T(4,128)} %stack.2078), calls=%async_computation.8 | async-start | bytes 524288 | tf_op jit(solution)/shard_map/all_to_all | solution.py:68
  396.4 2.9 copy-start.7
  412.3 13.9 %all-to-all-start.9 = ((f32[64,2,8,3]{2,1,3,0:T(2,128)}), f32[64,2,8,3]{2,1,3,0:T(2,128)S(1)}, u32[]{:S(2)}, u32[]{:S(2)}) async-start(f32[64,2,8,3]{2,1,3,0:T(2,128)} %copy.2985), calls=%async_computation.9 | async-start | bytes 393216 | tf_op jit(solution)/shard_map/all_to_all | solution.py:43
  437.0 7.4 %collective-permute-start.4 = (f32[256,3]{0,1:T(4,128)S(1)}, f32[256,3]{0,1:T(4,128)S(1)}, u32[]{:S(2)}, u32[]{:S(2)}) collective-permute-start(f32[256,3]{0,1:T(4,128)S(1)} %get-tuple-element.272), channel_id=1, source_target_pairs={{0,1},{1,2},{2,3},{3,4},{4,5},{5,6},{6,7},{7,8},{8,9},{9,10},{10,1... | collective-permute-start | bytes 9224 | tf_op jit(solution)/shard_map/ppermute | solution.py:23
  442.4 9.1 %collective-permute-start.5 = (f32[256,3]{0,1:T(4,128)S(1)}, f32[256,3]{0,1:T(4,128)S(1)}, u32[]{:S(2)}, u32[]{:S(2)}) collective-permute-start(f32[256,3]{0,1:T(4,128)S(1)} %get-tuple-element.273), channel_id=1, source_target_pairs={{1,0},{2,1},{3,2},{4,3},{5,4},{6,5},{7,6},{8,7},{9,8},{10,9},{11,1... | collective-permute-start | bytes 9224 | tf_op jit(solution)/shard_map/ppermute | solution.py:24
  551.6 4.9 copy-start.1
  556.7 4.6 collective-permute-start.6
  558.7 9.1 %collective-permute-start.7 = (f32[256,3]{0,1:T(4,128)S(1)}, f32[256,3]{0,1:T(4,128)S(1)}, u32[]{:S(2)}, u32[]{:S(2)}) collective-permute-start(f32[256,3]{0,1:T(4,128)S(1)} %get-tuple-element.271), channel_id=1, source_target_pairs={{1,0},{2,1},{3,2},{4,3},{5,4},{6,5},{7,6},{8,7},{9,8},{10,9},{11,1... | collective-permute-start | bytes 9224 | tf_op jit(solution)/shard_map/ppermute | solution.py:24
